TPU v7x, 32 devices: a whole 2x2x4 slice. The times are simulated.
32 devices in a mesh: row: 8 (over y, x, core), col: 4 (over z).
Axes of the slice: x: 2, y: 2, z: 4, core: 2. Of those that a mesh axis runs over, the one named last changes fastest.
Arguments:
- tokens: bfloat16 [6144, 2048], P('row', 'col'), may hold values from -6 to 6
- out_grad: bfloat16 [6144, 2048], P('row', 'col'), may hold values from -768 to 768
- counts: int32 [8], P('row'), may hold values from 65 to 768
- block_moves: int32 [4, 3], replicated, may hold values from 0 to 7, as said below
- segment_ids: int32 [6144], P('row'), may hold values from 0 to 191, never falling along the last dimension, each value on 1 to 128 neighbouring positions
- gate_weight: bfloat16 [2048, 8192], P('row', 'col'), may hold values from -0.125 to 0.125
- up_weight: bfloat16 [2048, 8192], P('row', 'col'), may hold values from -0.125 to 0.125
- down_weight: bfloat16 [2048, 8192], P('row', 'col'), may hold values from -0.0625 to 0.0625
Outputs:
- hidden: bfloat16 [4096, 8192], P('row', 'col')
- gate_grad: float32 [2048, 8192], P('row', 'col')
- up_grad: float32 [2048, 8192], P('row', 'col')
- down_grad: float32 [2048, 8192], P('row', 'col')
Inputs may be any that keep to these rules, and one draw needn't show every extreme that they name: `block_moves`: each row is (source rank, destination rank, block index); the block is a valid block of its source; no two rows share both source and destination, nor both source and block; a rank is the source of at most two rows or the destination of at most one, never both; after the moves every rank holds at most 4 valid blocks and some hold exactly 4. `segment_ids`: never falling along the whole array; each document covers 1 to 128 consecutive slots.
All inputs are finite; a program needn't handle non-finite values.
Results may differ from a plain program's by a relative error of at most 0.015.
Values may be sent and summed in bfloat16 or wider, within the bound.
A program may use at most 128 MiB of HBM per device.

v0:
```python
import jax
import jax.numpy as jnp
from jax import lax
from jax.sharding import PartitionSpec as P

BLOCK = 128
WORK = 4


def local_terms(gate_sum, up_sum, back_sum):
    logistic = jax.nn.sigmoid(gate_sum)
    activated = gate_sum * logistic
    hidden = (activated * up_sum).astype(jnp.bfloat16)
    gate_back = (back_sum * up_sum * logistic * (1.0 + gate_sum * (1.0 - logistic))).astype(
        jnp.bfloat16
    )
    up_back = (back_sum * activated).astype(jnp.bfloat16)
    return (hidden, gate_back, up_back)


def contract(left_side, right_side):
    return lax.dot_general(
        left_side, right_side, (((0,), (0,)), ((), ())), preferred_element_type=jnp.float32
    )


def on_device(
    tokens, out_grad, counts, block_moves, segment_ids, gate_weight, up_weight, down_weight
):
    ranks_all = lax.axis_size("row")
    me_rank = lax.axis_index("row")
    slot_rows = tokens.shape[0]
    cap_blocks = slot_rows // BLOCK
    feat_cols = tokens.shape[1]
    my_count = counts[0]
    places = jnp.arange(slot_rows, dtype=jnp.int32)
    following = jnp.concatenate([segment_ids[1:], segment_ids[-1:]])
    own_weight = ((places + 1 < my_count) & (following == segment_ids)).astype(jnp.float32)
    source = block_moves[:, 0]
    target = block_moves[:, 1]
    block_id = block_moves[:, 2]
    block_ids = jnp.arange(cap_blocks, dtype=jnp.int32)
    filled = (my_count + BLOCK - 1) // BLOCK
    moved_out = jnp.any(
        (source[None, :] == me_rank) & (block_id[None, :] == block_ids[:, None]), axis=1
    )
    kept_flag = (block_ids < filled) & jnp.logical_not(moved_out)
    arrive = target == me_rank
    flag_bits = jnp.concatenate([kept_flag, arrive]).astype(jnp.int32)
    local_ids = jnp.concatenate([block_ids, cap_blocks + source])
    list_place = jnp.cumsum(flag_bits) - 1
    slot_ids = jnp.arange(WORK, dtype=jnp.int32)
    slot_hit = (flag_bits[:, None] == 1) & (list_place[:, None] == slot_ids[None, :])
    slot_index = jnp.sum(jnp.where(slot_hit, local_ids[:, None] + 1, 0), axis=0) - 1
    peer_ids = jnp.arange(ranks_all, dtype=jnp.int32)
    outgoing = (source[None, :] == me_rank) & (target[None, :] == peer_ids[:, None])
    send_block = jnp.sum(jnp.where(outgoing, block_id[None, :], 0), axis=1)
    send_live = jnp.any(outgoing, axis=1)
    own_tokens = tokens.reshape(cap_blocks, BLOCK, feat_cols)
    own_grad = out_grad.reshape(cap_blocks, BLOCK, feat_cols)
    own_mask = own_weight.astype(jnp.bfloat16).reshape(cap_blocks, BLOCK)

    def outbox(block_rows):
        chosen = jnp.take(block_rows, send_block, axis=0)
        live_rows = send_live.reshape((-1,) + (1,) * (chosen.ndim - 1))
        return jnp.where(live_rows, chosen, jnp.zeros_like(chosen))

    whole_count = jnp.sum(own_weight).astype(jnp.int32)
    count_parts = jnp.broadcast_to(
        jnp.stack([whole_count // 256, whole_count % 256]).astype(jnp.bfloat16)[None, :],
        (ranks_all, 2),
    )
    got_tokens, got_grad, got_mask, got_parts = (
        lax.all_to_all(outbox(own_tokens), "row", split_axis=0, concat_axis=0, tiled=True),
        lax.all_to_all(outbox(own_grad), "row", split_axis=0, concat_axis=0, tiled=True),
        lax.all_to_all(outbox(own_mask), "row", split_axis=0, concat_axis=0, tiled=True),
        lax.all_to_all(count_parts, "row", split_axis=0, concat_axis=0, tiled=True),
    )
    part_values = got_parts.astype(jnp.float32)
    loss_total = 256.0 * jnp.sum(part_values[:, 0]) + jnp.sum(part_values[:, 1])

    def to_work(pool_rows):
        chosen = jnp.take(pool_rows, jnp.maximum(slot_index, 0), axis=0)
        live_rows = (slot_index >= 0).reshape((-1,) + (1,) * (chosen.ndim - 1))
        return jnp.where(live_rows, chosen, jnp.zeros_like(chosen))

    work_tokens = to_work(jnp.concatenate([own_tokens, got_tokens])).reshape(
        WORK * BLOCK, feat_cols
    )
    work_grad = to_work(jnp.concatenate([own_grad, got_grad])).reshape(WORK * BLOCK, feat_cols)
    work_mask = to_work(jnp.concatenate([own_mask, got_mask])).reshape(WORK * BLOCK)
    work_weight = work_mask.astype(jnp.float32)
    full_tokens, full_grad = (
        lax.all_gather(work_tokens, "col", axis=1, tiled=True),
        lax.all_gather(work_grad, "col", axis=1, tiled=True),
    )
    hidden_cols = gate_weight.shape[1]
    gate_piece = lax.all_gather(gate_weight, "row", axis=0, tiled=True)
    up_piece = lax.all_gather(up_weight, "row", axis=0, tiled=True)
    down_piece = lax.all_gather(down_weight, "row", axis=0, tiled=True)
    gate_sum = jnp.dot(full_tokens, gate_piece, preferred_element_type=jnp.float32)
    up_sum = jnp.dot(full_tokens, up_piece, preferred_element_type=jnp.float32)
    back_raw = jnp.dot(full_grad, down_piece, preferred_element_type=jnp.float32)
    back_sum = back_raw * work_weight[:, None]
    hidden, gate_back, up_back = local_terms(gate_sum, up_sum, back_sum)
    weighted = full_grad * work_mask[:, None]

    def term_rows(left_side, right_side):
        return contract(left_side, right_side) / loss_total

    down_grad = lax.psum_scatter(
        term_rows(weighted, hidden).astype(jnp.bfloat16), "row", scatter_dimension=0, tiled=True
    ).astype(jnp.float32)
    other_part = lax.psum_scatter(
        jnp.concatenate(
            [term_rows(full_tokens, gate_back), term_rows(full_tokens, up_back)], axis=1
        ).astype(jnp.bfloat16),
        "row",
        scatter_dimension=0,
        tiled=True,
    ).astype(jnp.float32)
    gate_grad = other_part[:, :hidden_cols]
    up_grad = other_part[:, hidden_cols:]
    return (hidden, gate_grad, up_grad, down_grad)


def solution(mesh):
    placed = (
        P("row", "col"),
        P("row", "col"),
        P("row"),
        P(),
        P("row"),
        P("row", "col"),
        P("row", "col"),
        P("row", "col"),
    )
    return jax.shard_map(
        on_device,
        mesh=mesh,
        in_specs=placed,
        out_specs=(P("row", "col"), P("row", "col"), P("row", "col"), P("row", "col")),
        check_vma=False,
    )
```

profile of v0, /device:TPU:0, one launch (start us, length us, event | category | flops | bytes accessed | tf_op | source)
XLA Modules:
  0.0 525.0 jit_solution(14892905460877287616)
XLA Ops:
  7.2 1.0 fusion.22
  8.6 1.7 gather_fusion.4
  10.3 1.7 gather_fusion.2
  12.1 1.6 select_select_fusion
  13.7 5.3 %all-to-all-start = ((bf16[8,128,512]{2,1,0:T(8,128)(2,1)}), bf16[8,128,512]{2,1,0:T(8,128)(2,1)S(1)}, u32[]{:S(2)}, u32[]{:S(2)}) async-start(bf16[8,128,512]{2,1,0:T(8,128)(2,1)} %get-tuple-element.40), calls=%async_computation | async-start | bytes 2097152 | tf_op jit(solution)/shard_map/all_to_all | solution.py:74
  20.2 14.2 %all-to-all-done = bf16[8,128,512]{2,1,0:T(8,128)(2,1)S(1)} async-done(((bf16[8,128,512]{2,1,0:T(8,128)(2,1)}), bf16[8,128,512]{2,1,0:T(8,128)(2,1)S(1)}, u32[]{:S(2)}, u32[]{:S(2)}) %all-to-all-start) | async-done | bytes 1048608 | tf_op jit(solution)/shard_map/all_to_all | solution.py:74
  34.4 4.2 all-to-all-start.1
  38.9 1.4 pad_maximum_fusion.1
  40.3 2.1 gather_fusion.3
  42.4 11.6 %all-to-all-done.1 = bf16[8,128,512]{2,1,0:T(8,128)(2,1)} async-done(((bf16[8,128,512]{2,1,0:T(8,128)(2,1)}), bf16[8,128,512]{2,1,0:T(8,128)(2,1)}, u32[]{:S(2)}, u32[]{:S(2)}) %all-to-all-start.1) | async-done | bytes 1048608 | tf_op jit(solution)/shard_map/all_to_all | solution.py:75
  54.0 1.4 pad_maximum_fusion.2
  55.4 0.6 gather_fusion.5
  56.0 1.1 select_select_fusion.2
  57.2 0.7 all-gather.8.cloned.1.call-update
  58.0 0.7 all-gather.10.cloned.1.call-update
  58.7 0.5 all-gather.12.cloned.1.call-update
  59.3 0.5 all-gather.14.cloned.1.call-update
  59.9 0.6 slice.31
  60.5 0.7 fusion.8
  61.2 0.6 convert_reduce_fusion
  62.6 0.6 broadcast_in_dim.133
  63.2 3.3 all-to-all-start.3
  66.6 0.6 gather_fusion
  67.2 0.6 copy.44
  67.8 3.3 all-to-all-done.3
  71.1 3.3 all-to-all-start.2
  74.7 0.6 slice_reduce_fusion.1
  76.6 2.4 all-to-all-done.2
  79.0 0.6 gather_fusion.1
  79.6 22.8 %all-gather.6.cloned.1.call-done = bf16[512,2048]{1,0:T(8,128)(2,1)} async-done(((bf16[512,512]{1,0:T(8,128)(2,1)}), bf16[512,2048]{1,0:T(8,128)(2,1)}) %all-gather.6.cloned.1.call-update) | async-done | bytes 2097168 | tf_op jit(solution)/shard_map/all_gather | solution.py:94
  102.4 55.0 %all-gather.8.cloned.1.call-done = bf16[2048,2048]{1,0:T(8,128)(2,1)} async-done(((bf16[256,2048]{1,0:T(8,128)(2,1)}), bf16[2048,2048]{1,0:T(8,128)(2,1)}) %all-gather.8.cloned.1.call-update) | async-done | bytes 8388624 | tf_op jit(solution)/shard_map/all_gather | solution.py:98
  157.4 10.5 %fusion.23 = f32[512,2048]{1,0:T(8,128)} fusion(bf16[512,2048]{1,0:T(8,128)(2,1)} %all-gather.6.cloned.1.call-done, bf16[2048,2048]{1,0:T(8,128)(2,1)} %all-gather.8.cloned.1.call-done), kind=kOutput, calls=%fused_computation.76 | convolution fusion | flops 4294967296 | bytes 14680064 | tf_op jit(solution)/shard_map/dot_general | solution.py:101
  167.9 45.7 %all-gather.10.cloned.1.call-done = bf16[2048,2048]{1,0:T(8,128)(2,1)} async-done(((bf16[256,2048]{1,0:T(8,128)(2,1)}), bf16[2048,2048]{1,0:T(8,128)(2,1)}) %all-gather.10.cloned.1.call-update) | async-done | bytes 8388624 | tf_op jit(solution)/shard_map/all_gather | solution.py:99
  213.6 10.9 %multiply_convert_fusion.2 = (bf16[512,2048]{1,0:T(8,128)(2,1)}, f32[512,2048]{1,0:T(8,128)}) fusion(f32[512,2048]{1,0:T(8,128)} %fusion.23, bf16[512,2048]{1,0:T(8,128)(2,1)S(1)} %copy-done.3, bf16[2048,2048]{1,0:T(8,128)(2,1)} %all-gather.10.cloned.1.call-done), kind=kOutput, calls=%fused_computation.12 | convolution fusion | flops 4301258752 | bytes 20971520 | tf_op jit(solution)/shard_map/dot_general | solution.py:102
  224.5 36.8 %all-gather.12.cloned.1.call-done = bf16[512,2048]{1,0:T(8,128)(2,1)} async-done(((bf16[512,512]{1,0:T(8,128)(2,1)}), bf16[512,2048]{1,0:T(8,128)(2,1)}) %all-gather.12.cloned.1.call-update) | async-done | bytes 2097168 | tf_op jit(solution)/shard_map/all_gather | solution.py:95
  261.3 10.5 %divide_convert_fusion = bf16[2048,2048]{0,1:T(8,128)(2,1)} fusion(f32[]{:T(128)S(6)} %add.97, bf16[512,2048]{1,0:T(8,128)(2,1)} %get-tuple-element.43, bf16[512,2048]{1,0:T(8,128)(2,1)} %all-gather.12.cloned.1.call-done, bf16[512]{0:T(512)(128)(2,1)S(1)} %get-tuple-element.29), kind=kOutput, calls=%fused_computation.7 | convolution fusion | flops 4304404480 | bytes 12583940 | tf_op jit(solution)/shard_map/dot_general | solution.py:22
  272.0 44.1 %all-gather.14.cloned.1.call-done = bf16[2048,2048]{1,0:T(8,128)(2,1)} async-done(((bf16[256,2048]{1,0:T(8,128)(2,1)}), bf16[2048,2048]{1,0:T(8,128)(2,1)}) %all-gather.14.cloned.1.call-update) | async-done | bytes 8388624 | tf_op jit(solution)/shard_map/all_gather | solution.py:100
  316.1 7.7 %fusion.24 = f32[512,2048]{1,0:T(8,128)S(1)} fusion(bf16[512,2048]{1,0:T(8,128)(2,1)} %all-gather.12.cloned.1.call-done, bf16[2048,2048]{1,0:T(8,128)(2,1)} %all-gather.14.cloned.1.call-done), kind=kOutput, calls=%fused_computation.77 | convolution fusion | flops 4294967296 | bytes 14680064 | tf_op jit(solution)/shard_map/dot_general | solution.py:103
  323.8 2.1 copy-done.5
  325.9 8.0 %divide_convert_fusion.2 = bf16[2048,2048]{0,1:T(8,128)(2,1)S(1)} fusion(f32[]{:T(128)S(6)} %add.97, bf16[512,2048]{1,0:T(8,128)(2,1)S(1)} %copy-done.3, f32[512,2048]{1,0:T(8,128)S(1)} %copy-done.4, f32[512,2048]{1,0:T(8,128)} %get-tuple-element.44, f32[512,2048]{1,0:T(8,128)S(1)} %fusion.24, f32[512]{0:T(512)S(1)} %get-tuple-element.28), kind=kOutput, calls=%fused_computation.9 | convolution fusion | flops 4314890240 | bytes 23070724 | tf_op jit(solution)/shard_map/dot_general | solution.py:22
  333.8 10.9 %divide_convert_fusion.1 = bf16[2048,2048]{0,1:T(8,128)(2,1)} fusion(f32[]{:T(128)S(6)} %add.97, bf16[512,2048]{1,0:T(8,128)(2,1)S(1)} %copy-done.3, f32[512,2048]{1,0:T(8,128)} %copy-done.5, f32[512]{0:T(512)S(1)} %get-tuple-element.28, f32[512,2048]{1,0:T(8,128)S(1)} %copy-done.4), kind=kOutput, calls=%fused_computation.8 | convolution fusion | flops 4310695936 | bytes 18876420 | tf_op jit(solution)/shard_map/dot_general | solution.py:22
  344.7 10.8 %pad_maximum_fusion = bf16[2048,4096]{0,1:T(8,128)(2,1)} fusion(bf16[2048,2048]{0,1:T(8,128)(2,1)} %divide_convert_fusion.1, bf16[2048,2048]{0,1:T(8,128)(2,1)S(1)} %divide_convert_fusion.2), kind=kLoop, calls=%fused_computation.6 | loop fusion | flops 33554432 | bytes 33554432 | tf_op jit(solution)/shard_map/concatenate | solution.py:115
  355.5 35.2 %reduce-scatter.5.cloned.1.call-done = bf16[256,2048]{0,1:T(8,128)(2,1)} async-done(((bf16[2048,2048]{0,1:T(8,128)(2,1)}), bf16[256,2048]{0,1:T(8,128)(2,1)}) %reduce-scatter.5.cloned.1.call-update) | async-done | bytes 1048592 | tf_op jit(solution)/shard_map/reduce_scatter | solution.py:111
  390.7 2.6 copy.49
  393.3 117.0 %reduce-scatter.3.cloned.1.call-done = bf16[256,4096]{0,1:T(8,128)(2,1)} async-done(((bf16[2048,4096]{0,1:T(8,128)(2,1)}), bf16[256,4096]{0,1:T(8,128)(2,1)}) %reduce-scatter.3.cloned.1.call-update) | async-done | bytes 2097168 | tf_op jit(solution)/shard_map/reduce_scatter | solution.py:114
  510.3 3.2 fusion.21
  513.5 2.9 copy.48
  516.4 1.8 copy.47
  (55 shorter events, 2.3 us)
Async XLA Ops:
  12.1 26.9 %copy-start = (bf16[768,512]{1,0:T(8,128)(2,1)S(1)}, bf16[768,512]{1,0:T(8,128)(2,1)}, u32[]{:S(2)}) copy-start(bf16[768,512]{1,0:T(8,128)(2,1)} %param.12) | copy-start | bytes 2359300
  13.7 40.3 %copy-start.1 = (bf16[768,512]{1,0:T(8,128)(2,1)S(1)}, bf16[768,512]{1,0:T(8,128)(2,1)}, u32[]{:S(2)}) copy-start(bf16[768,512]{1,0:T(8,128)(2,1)} %param.13) | copy-start | bytes 2359300
  13.7 20.7 %all-to-all-start = ((bf16[8,128,512]{2,1,0:T(8,128)(2,1)}), bf16[8,128,512]{2,1,0:T(8,128)(2,1)S(1)}, u32[]{:S(2)}, u32[]{:S(2)}) async-start(bf16[8,128,512]{2,1,0:T(8,128)(2,1)} %get-tuple-element.40), calls=%async_computation | async-start | bytes 2097152 | tf_op jit(solution)/shard_map/all_to_all | solution.py:74
  34.4 19.6 %all-to-all-start.1 = ((bf16[8,128,512]{2,1,0:T(8,128)(2,1)}), bf16[8,128,512]{2,1,0:T(8,128)(2,1)}, u32[]{:S(2)}, u32[]{:S(2)}) async-start(bf16[8,128,512]{2,1,0:T(8,128)(2,1)} %get-tuple-element.39), calls=%async_computation.1 | async-start | bytes 2097152 | tf_op jit(solution)/shard_map/all_to_all | solution.py:75
  38.6 63.8 %all-gather.6.cloned.1.call-start = ((), (), s32[]{:S(2)}) async-start(), calls=%async_computation.6 | async-start | bytes 2621440 | tf_op jit(solution)/shard_map/all_gather | solution.py:94
  55.4 4.4 copy-start.2
  57.2 100.2 %all-gather.8.cloned.1.call-start = ((), (), s32[]{:S(2)}) async-start(), calls=%async_computation.7 | async-start | bytes 9437184 | tf_op jit(solution)/shard_map/all_gather | solution.py:98
  58.0 155.6 %all-gather.10.cloned.1.call-start = ((), (), s32[]{:S(2)}) async-start(), calls=%async_computation.8 | async-start | bytes 9437184 | tf_op jit(solution)/shard_map/all_gather | solution.py:99
  58.7 202.6 %all-gather.12.cloned.1.call-start = ((), (), s32[]{:S(2)}) async-start(), calls=%async_computation.9 | async-start | bytes 2621440 | tf_op jit(solution)/shard_map/all_gather | solution.py:95
  59.3 256.8 %all-gather.14.cloned.1.call-start = ((), (), s32[]{:S(2)}) async-start(), calls=%async_computation.10 | async-start | bytes 9437184 | tf_op jit(solution)/shard_map/all_gather | solution.py:100
  63.2 7.9 %all-to-all-start.3 = ((bf16[8,1,2]{2,1,0:T(2,128)(2,1)}), bf16[8,1,2]{2,1,0:T(2,128)(2,1)S(1)}, u32[]{:S(2)}, u32[]{:S(2)}) async-start(bf16[8,1,2]{2,1,0:T(2,128)(2,1)} %broadcast_in_dim.133), calls=%async_computation.3 | async-start | bytes 8192 | tf_op jit(solution)/shard_map/all_to_all | solution.py:77
  71.1 7.9 %all-to-all-start.2 = ((bf16[8,1,128]{2,1,0:T(2,128)(2,1)}), bf16[8,1,128]{2,1,0:T(2,128)(2,1)S(1)}, u32[]{:S(2)}, u32[]{:S(2)}) async-start(bf16[8,1,128]{2,1,0:T(2,128)(2,1)} %copy.44), calls=%async_computation.2 | async-start | bytes 8192 | tf_op jit(solution)/shard_map/all_to_all | solution.py:76
  74.4 316.3 %reduce-scatter.5.cloned.1.call-start = ((), (), s32[]{:S(2)}) async-start(), calls=%async_computation.12 | async-start | bytes 9437184 | tf_op jit(solution)/shard_map/reduce_scatter | solution.py:111
  102.4 111.2 %copy-start.3 = (bf16[512,2048]{1,0:T(8,128)(2,1)S(1)}, bf16[512,2048]{1,0:T(8,128)(2,1)}, u32[]{:S(2)}) copy-start(bf16[512,2048]{1,0:T(8,128)(2,1)} %all-gather.6.cloned.1.call-done) | copy-start | bytes 6291460
  271.7 238.6 %reduce-scatter.3.cloned.1.call-start = ((), (), s32[]{:S(2)}) async-start(), calls=%async_computation.11 | async-start | bytes 18874368 | tf_op jit(solution)/shard_map/reduce_scatter | solution.py:114
  316.1 9.8 %copy-start.4 = (f32[512,2048]{1,0:T(8,128)S(1)}, f32[512,2048]{1,0:T(8,128)}, u32[]{:S(2)}) copy-start(f32[512,2048]{1,0:T(8,128)} %fusion.23) | copy-start | bytes 12582916
  323.8 2.1 copy-start.5
Sparse Core Ops, SparseCore 0:
  57.3 45.0 all-gather.5
  104.3 53.0 all-gather.7
  159.3 54.2 all-gather.9
  215.6 45.6 all-gather.11
  263.0 53.0 all-gather.13
  319.4 71.2 reduce-scatter.4
  394.3 115.9 reduce-scatter.2
where the time goes:
time: 526 us; the launch traced here: 525 us
  waiting for transfers between devices  391 us (74%)
  matrix products  58.4 us (11%)
  local copies, waits for them, and re-layouts  22.9 us (4%)
  other arithmetic  19.4 us (4%)
  starting transfers between devices  16.9 us (3%)
  between operations  16.9 us (3%)
    reduce_scatter x1, waiting for transfers between devices, on_device(): lax.psum_scatter(jnp.concatenate([term_rows(full_tokens, gate_back), term...  117 us
    all_gather x1, waiting for transfers between devices, on_device(): gate_piece = lax.all_gather(gate_weight, 'row', axis=0, tiled=True)  55 us
    all_gather x1, waiting for transfers between devices, on_device(): up_piece = lax.all_gather(up_weight, 'row', axis=0, tiled=True)  45.7 us
    all_gather x1, waiting for transfers between devices, on_device(): down_piece = lax.all_gather(down_weight, 'row', axis=0, tiled=True)  44.1 us
    all_gather x1, waiting for transfers between devices, on_device(): lax.all_gather(work_grad, 'col', axis=1, tiled=True)  36.8 us
    reduce_scatter x1, waiting for transfers between devices, on_device(): lax.psum_scatter(term_rows(weighted, hidden).astype(jnp.bfloat16), 'row',...  35.2 us
    dot_general x3, matrix products, contract(): lax.dot_general(left_side, right_side, (((0,), (0,)), ((), ())), preferre...  29.3 us
    all_gather x1, waiting for transfers between devices, on_device(): lax.all_gather(work_tokens, 'col', axis=1, tiled=True)  22.8 us
  transfers between devices with their start and end apart: 11, of which 11 were waited for; matrix products, arithmetic and copies ran while one was open for 15% of the time, Pallas kernels for 0%

commit v1 on v0

--- a/solution.py
+++ b/solution.py
@@ -97,7 +97,22 @@
     hidden_cols = gate_weight.shape[1]
     gate_piece = lax.all_gather(gate_weight, "row", axis=0, tiled=True)
     up_piece = lax.all_gather(up_weight, "row", axis=0, tiled=True)
-    down_piece = lax.all_gather(down_weight, "row", axis=0, tiled=True)
+
+    def set_shards_all(panel):
+        bus_axis = "row"
+        n_parts = lax.axis_size(bus_axis)
+        pile = [(i, (i + 1) % n_parts) for i in range(n_parts)]
+
+        def process_shapes(new):
+            if len(new) == n_parts:
+                return new
+            return process_shapes([lax.ppermute(new[0], bus_axis, pile), *new])
+
+        z1 = process_shapes([panel])
+        near = jnp.concatenate(z1, axis=0)
+        return jnp.roll(near, (lax.axis_index(bus_axis) + 1) * panel.shape[0], 0)
+
+    down_piece = set_shards_all(down_weight)
     gate_sum = jnp.dot(full_tokens, gate_piece, preferred_element_type=jnp.float32)
     up_sum = jnp.dot(full_tokens, up_piece, preferred_element_type=jnp.float32)
     back_raw = jnp.dot(full_grad, down_piece, preferred_element_type=jnp.float32)

time: 526 us -> 500 us (0.951)
  waiting for transfers between devices: 391 us -> 344 us
  local copies, waits for them, and re-layouts: 22.9 us -> 37.8 us
    ppermute x0 -> x7, waiting for transfers between devices: none -> 97.5 us  [process_shapes(): return process_shapes([lax.ppermute(new[0], bus_axis, pile), *new])]
    all_gather x1, waiting for transfers between devices: 55 us -> 0.01 us  [on_device(): gate_piece = lax.all_gather(gate_weight, 'row', axis=0, tiled=True)]
    all_gather x1 -> x0, waiting for transfers between devices: 44.1 us -> none  [on_device(): down_piece = lax.all_gather(down_weight, 'row', axis=0, tiled=True)]
    all_gather x1, waiting for transfers between devices: 22.8 us -> 0.01 us  [on_device(): lax.all_gather(work_tokens, 'col', axis=1, tiled=True)]
    reduce_scatter x1, waiting for transfers between devices: 35.2 us -> 18.8 us  [on_device(): lax.psum_scatter(term_rows(weighted, hidden).astype(jnp.bfloat16), 'row',...]
    unnamed x18 -> x41, local copies, waits for them, and re-layouts: 9.54 us -> 22.8 us
    all_to_all x1, waiting for transfers between devices: 2.38 us -> 9.2 us  [on_device(): lax.all_to_all(outbox(own_mask), 'row', split_axis=0, concat_axis=0, tile...]
    all_gather x1, waiting for transfers between devices: 45.7 us -> 39.9 us  [on_device(): up_piece = lax.all_gather(up_weight, 'row', axis=0, tiled=True)]
  transfers between devices with their start and end apart: 11 -> 17, of which waited for: 11 -> 12; matrix products, arithmetic and copies ran while one was open for 15% -> 19% of each run, Pallas kernels for 0% -> 0%
where the time goes in v1:
time: 500 us; the launch traced here: 498 us
  waiting for transfers between devices  344 us (69%)
  matrix products  60.4 us (12%)
  local copies, waits for them, and re-layouts  37.8 us (8%)
  other arithmetic  20.5 us (4%)
  starting transfers between devices  18.2 us (4%)
  between operations  17 us (3%)
    reduce_scatter x1, waiting for transfers between devices, on_device(): lax.psum_scatter(jnp.concatenate([term_rows(full_tokens, gate_back), term...  117 us
    ppermute x7, waiting for transfers between devices, process_shapes(): return process_shapes([lax.ppermute(new[0], bus_axis, pile), *new])  97.5 us
    all_gather x1, waiting for transfers between devices, on_device(): up_piece = lax.all_gather(up_weight, 'row', axis=0, tiled=True)  39.9 us
    all_gather x1, waiting for transfers between devices, on_device(): lax.all_gather(work_grad, 'col', axis=1, tiled=True)  35 us
    dot_general x3, matrix products, contract(): lax.dot_general(left_side, right_side, (((0,), (0,)), ((), ())), preferre...  30.8 us
    unnamed x41, local copies, waits for them, and re-layouts  22.8 us
    reduce_scatter x1, waiting for transfers between devices, on_device(): lax.psum_scatter(term_rows(weighted, hidden).astype(jnp.bfloat16), 'row',...  18.8 us
    all_to_all x1, waiting for transfers between devices, on_device(): lax.all_to_all(outbox(own_tokens), 'row', split_axis=0, concat_axis=0, ti...  14.2 us
  transfers between devices with their start and end apart: 17, of which 12 were waited for; matrix products, arithmetic and copies ran while one was open for 19% of the time, Pallas kernels for 0%

profile of v1, /device:TPU:0, one launch (start us, length us, event | category | flops | bytes accessed | tf_op | source)
XLA Modules:
  0.0 498.3 jit_solution(13661178069624658935)
XLA Ops:
  7.2 1.0 fusion.25
  8.5 1.7 gather_fusion.2
  10.3 1.7 gather_fusion.4
  12.1 1.6 select_select_fusion
  13.7 5.3 %all-to-all-start = ((bf16[8,128,512]{2,1,0:T(8,128)(2,1)}), bf16[8,128,512]{2,1,0:T(8,128)(2,1)S(1)}, u32[]{:S(2)}, u32[]{:S(2)}) async-start(bf16[8,128,512]{2,1,0:T(8,128)(2,1)} %get-tuple-element.40), calls=%async_computation | async-start | bytes 2097152 | tf_op jit(solution)/shard_map/all_to_all | solution.py:74
  20.2 14.2 %all-to-all-done = bf16[8,128,512]{2,1,0:T(8,128)(2,1)S(1)} async-done(((bf16[8,128,512]{2,1,0:T(8,128)(2,1)}), bf16[8,128,512]{2,1,0:T(8,128)(2,1)S(1)}, u32[]{:S(2)}, u32[]{:S(2)}) %all-to-all-start) | async-done | bytes 1048608 | tf_op jit(solution)/shard_map/all_to_all | solution.py:74
  34.4 4.2 all-to-all-start.1
  39.0 1.4 pad_maximum_fusion.1
  40.3 2.1 gather_fusion.3
  42.5 11.6 %all-to-all-done.1 = bf16[8,128,512]{2,1,0:T(8,128)(2,1)} async-done(((bf16[8,128,512]{2,1,0:T(8,128)(2,1)}), bf16[8,128,512]{2,1,0:T(8,128)(2,1)}, u32[]{:S(2)}, u32[]{:S(2)}) %all-to-all-start.1) | async-done | bytes 1048608 | tf_op jit(solution)/shard_map/all_to_all | solution.py:75
  54.0 2.6 pad_maximum_fusion.2
  56.7 2.1 gather_fusion.5
  58.7 1.1 select_select_fusion.2
  60.0 0.7 all-gather.7.cloned.1.call-update
  61.5 15.1 %collective-permute-done = bf16[256,2048]{1,0:T(8,128)(2,1)S(1)} collective-permute-done((bf16[256,2048]{1,0:T(8,128)(2,1)S(1)}, bf16[256,2048]{1,0:T(8,128)(2,1)S(1)}, u32[]{:S(2)}, u32[]{:S(2)}) %collective-permute-start) | collective-permute-done | bytes 1048608 | tf_op jit(solution)/shard_map/ppermute | solution.py:109
  76.6 15.1 %collective-permute-done.1 = bf16[256,2048]{1,0:T(8,128)(2,1)S(1)} collective-permute-done((bf16[256,2048]{1,0:T(8,128)(2,1)S(1)}, bf16[256,2048]{1,0:T(8,128)(2,1)S(1)}, u32[]{:S(2)}, u32[]{:S(2)}) %collective-permute-start.1) | collective-permute-done | bytes 1048608 | tf_op jit(solution)/shard_map/ppermute | solution.py:109
  91.7 1.0 copy-done.3
  92.7 15.1 %collective-permute-done.2 = bf16[256,2048]{1,0:T(8,128)(2,1)S(1)} collective-permute-done((bf16[256,2048]{1,0:T(8,128)(2,1)S(1)}, bf16[256,2048]{1,0:T(8,128)(2,1)S(1)}, u32[]{:S(2)}, u32[]{:S(2)}) %collective-permute-start.2) | collective-permute-done | bytes 1048608 | tf_op jit(solution)/shard_map/ppermute | solution.py:109
  107.8 1.0 copy-done.5
  108.8 26.5 %collective-permute-done.3 = bf16[256,2048]{1,0:T(8,128)(2,1)} collective-permute-done((bf16[256,2048]{1,0:T(8,128)(2,1)S(1)}, bf16[256,2048]{1,0:T(8,128)(2,1)}, u32[]{:S(2)}, u32[]{:S(2)}) %collective-permute-start.3) | collective-permute-done | bytes 1048608 | tf_op jit(solution)/shard_map/ppermute | solution.py:109
  138.5 3.9 all-to-all-start.3
  142.4 25.7 %collective-permute-done.4 = bf16[256,2048]{1,0:T(8,128)(2,1)} collective-permute-done((bf16[256,2048]{1,0:T(8,128)(2,1)}, bf16[256,2048]{1,0:T(8,128)(2,1)}, u32[]{:S(2)}, u32[]{:S(2)}) %collective-permute-start.4) | collective-permute-done | bytes 1048608 | tf_op jit(solution)/shard_map/ppermute | solution.py:109
  169.3 3.9 all-to-all-start.2
  175.3 9.2 %all-to-all-done.2 = bf16[8,1,128]{2,1,0:T(2,128)(2,1)S(1)} async-done(((bf16[8,1,128]{2,1,0:T(2,128)(2,1)}), bf16[8,1,128]{2,1,0:T(2,128)(2,1)S(1)}, u32[]{:S(2)}, u32[]{:S(2)}) %all-to-all-start.2) | async-done | bytes 2080 | tf_op jit(solution)/shard_map/all_to_all | solution.py:76
  185.5 10.8 %fusion.26 = f32[512,2048]{1,0:T(8,128)} fusion(bf16[512,2048]{1,0:T(8,128)(2,1)} %all-gather.5.cloned.1.call-done, bf16[2048,2048]{1,0:T(8,128)(2,1)} %all-gather.7.cloned.1.call-done), kind=kOutput, calls=%fused_computation.95 | convolution fusion | flops 4294967296 | bytes 14680064 | tf_op jit(solution)/shard_map/dot_general | solution.py:116
  196.3 39.9 %all-gather.9.cloned.1.call-done = bf16[2048,2048]{1,0:T(8,128)(2,1)} async-done(((bf16[256,2048]{1,0:T(8,128)(2,1)}), bf16[2048,2048]{1,0:T(8,128)(2,1)}) %all-gather.9.cloned.1.call-update) | async-done | bytes 8388624 | tf_op jit(solution)/shard_map/all_gather | solution.py:99
  236.1 12.7 %multiply_convert_fusion.2 = (bf16[512,2048]{1,0:T(8,128)(2,1)}, f32[512,2048]{1,0:T(8,128)}) fusion(f32[512,2048]{1,0:T(8,128)} %fusion.26, bf16[512,2048]{1,0:T(8,128)(2,1)} %all-gather.5.cloned.1.call-done, bf16[2048,2048]{1,0:T(8,128)(2,1)} %all-gather.9.cloned.1.call-done), kind=kOutput, calls=%fused_computation.14 | convolution fusion | flops 4301258752 | bytes 20971520 | tf_op jit(solution)/shard_map/dot_general | solution.py:117
  248.8 35.0 %all-gather.11.cloned.1.call-done = bf16[512,2048]{1,0:T(8,128)(2,1)} async-done(((bf16[512,512]{1,0:T(8,128)(2,1)}), bf16[512,2048]{1,0:T(8,128)(2,1)}) %all-gather.11.cloned.1.call-update) | async-done | bytes 2097168 | tf_op jit(solution)/shard_map/all_gather | solution.py:95
  283.8 10.1 %divide_convert_fusion = bf16[2048,2048]{0,1:T(8,128)(2,1)} fusion(f32[]{:T(128)S(6)} %add.113, bf16[512,2048]{1,0:T(8,128)(2,1)} %get-tuple-element.43, bf16[512,2048]{1,0:T(8,128)(2,1)} %all-gather.11.cloned.1.call-done, bf16[512]{0:T(512)(128)(2,1)S(1)} %get-tuple-element.29), kind=kOutput, calls=%fused_computation.7 | convolution fusion | flops 4304404480 | bytes 12583940 | tf_op jit(solution)/shard_map/dot_general | solution.py:22
  294.2 1.4 constant_dynamic-update-slice_fusion.15
  295.6 1.4 constant_dynamic-update-slice_fusion.14
  297.0 1.3 constant_dynamic-update-slice_fusion.13
  298.3 1.3 constant_dynamic-update-slice_fusion.12
  300.0 1.5 constant_dynamic-update-slice_fusion.7
  301.5 1.5 constant_dynamic-update-slice_fusion.6
  303.0 1.5 constant_dynamic-update-slice_fusion.5
  304.5 1.4 constant_dynamic-update-slice_fusion.4
  306.2 1.6 copy-done.9
  307.8 6.1 %fusion = f32[512,2048]{1,0:T(8,128)} fusion(bf16[512,2048]{1,0:T(8,128)(2,1)S(1)} %copy-done.9, bf16[4096,2048]{1,0:T(8,128)(2,1)S(1)} %constant_dynamic-update-slice_fusion, s32[]{:T(128)S(6)} %select_n.137), kind=kOutput, calls=%fused_computation.10 | convolution fusion | flops 4294967296 | bytes 14680068 | tf_op jit(solution)/shard_map/dot_general | solution.py:118
  314.0 8.8 %divide_convert_fusion.2 = bf16[2048,2048]{0,1:T(8,128)(2,1)S(1)} fusion(f32[]{:T(128)S(6)} %add.113, bf16[512,2048]{1,0:T(8,128)(2,1)S(1)} %copy-done.8, f32[512,2048]{1,0:T(8,128)} %fusion.26, f32[512,2048]{1,0:T(8,128)} %get-tuple-element.44, f32[512,2048]{1,0:T(8,128)} %fusion, f32[512]{0:T(512)S(1)} %get-tuple-element.28), kind=kOutput, calls=%fused_computation.9 | convolution fusion | flops 4314890240 | bytes 23070724 | tf_op jit(solution)/shard_map/dot_general | solution.py:22
  322.8 11.9 %divide_convert_fusion.1 = bf16[2048,2048]{0,1:T(8,128)(2,1)} fusion(f32[]{:T(128)S(6)} %add.113, bf16[512,2048]{1,0:T(8,128)(2,1)S(1)} %copy-done.8, f32[512,2048]{1,0:T(8,128)} %fusion, f32[512]{0:T(512)S(1)} %get-tuple-element.28, f32[512,2048]{1,0:T(8,128)} %fusion.26), kind=kOutput, calls=%fused_computation.8 | convolution fusion | flops 4310695936 | bytes 18876420 | tf_op jit(solution)/shard_map/dot_general | solution.py:22
  334.7 10.6 %pad_maximum_fusion = bf16[2048,4096]{0,1:T(8,128)(2,1)} fusion(bf16[2048,2048]{0,1:T(8,128)(2,1)} %divide_convert_fusion.1, bf16[2048,2048]{0,1:T(8,128)(2,1)S(1)} %divide_convert_fusion.2), kind=kLoop, calls=%fused_computation.6 | loop fusion | flops 33554432 | bytes 33554432 | tf_op jit(solution)/shard_map/concatenate | solution.py:130
  345.4 18.8 %reduce-scatter.5.cloned.1.call-done = bf16[256,2048]{0,1:T(8,128)(2,1)} async-done(((bf16[2048,2048]{0,1:T(8,128)(2,1)}), bf16[256,2048]{0,1:T(8,128)(2,1)}) %reduce-scatter.5.cloned.1.call-update) | async-done | bytes 1048592 | tf_op jit(solution)/shard_map/reduce_scatter | solution.py:126
  364.1 2.6 copy.49
  366.7 116.9 %reduce-scatter.3.cloned.1.call-done = bf16[256,4096]{0,1:T(8,128)(2,1)} async-done(((bf16[2048,4096]{0,1:T(8,128)(2,1)}), bf16[256,4096]{0,1:T(8,128)(2,1)}) %reduce-scatter.3.cloned.1.call-update) | async-done | bytes 2097168 | tf_op jit(solution)/shard_map/reduce_scatter | solution.py:129
  483.6 3.2 fusion.24
  486.8 2.9 copy.47
  489.7 1.8 copy.48
  (90 shorter events, 8.5 us)
Async XLA Ops:
  12.1 26.9 %copy-start = (bf16[768,512]{1,0:T(8,128)(2,1)S(1)}, bf16[768,512]{1,0:T(8,128)(2,1)}, u32[]{:S(2)}) copy-start(bf16[768,512]{1,0:T(8,128)(2,1)} %param.12) | copy-start | bytes 2359300
  13.7 40.4 %copy-start.1 = (bf16[768,512]{1,0:T(8,128)(2,1)S(1)}, bf16[768,512]{1,0:T(8,128)(2,1)}, u32[]{:S(2)}) copy-start(bf16[768,512]{1,0:T(8,128)(2,1)} %param.13) | copy-start | bytes 2359300
  13.7 20.7 %all-to-all-start = ((bf16[8,128,512]{2,1,0:T(8,128)(2,1)}), bf16[8,128,512]{2,1,0:T(8,128)(2,1)S(1)}, u32[]{:S(2)}, u32[]{:S(2)}) async-start(bf16[8,128,512]{2,1,0:T(8,128)(2,1)} %get-tuple-element.40), calls=%async_computation | async-start | bytes 2097152 | tf_op jit(solution)/shard_map/all_to_all | solution.py:74
  34.4 19.6 %all-to-all-start.1 = ((bf16[8,128,512]{2,1,0:T(8,128)(2,1)}), bf16[8,128,512]{2,1,0:T(8,128)(2,1)}, u32[]{:S(2)}, u32[]{:S(2)}) async-start(bf16[8,128,512]{2,1,0:T(8,128)(2,1)} %get-tuple-element.39), calls=%async_computation.1 | async-start | bytes 2097152 | tf_op jit(solution)/shard_map/all_to_all | solution.py:75
  38.7 146.8 %all-gather.5.cloned.1.call-start = ((), (), s32[]{:S(2)}) async-start(), calls=%async_computation.6 | async-start | bytes 2621440 | tf_op jit(solution)/shard_map/all_gather | solution.py:94
  42.4 19.0 %copy-start.2 = (bf16[256,2048]{1,0:T(8,128)(2,1)S(1)}, bf16[256,2048]{1,0:T(8,128)(2,1)}, u32[]{:S(2)}) copy-start(bf16[256,2048]{1,0:T(8,128)(2,1)} %param.19) | copy-start | bytes 3145732
  42.4 92.8 %copy-start.7 = (s32[768]{0:T(1024)S(1)}, s32[768]{0:T(1024)}, u32[]{:S(2)}) copy-start(s32[768]{0:T(1024)} %param.16) | copy-start | bytes 9220
  59.9 125.6 %all-gather.7.cloned.1.call-start = ((), (), s32[]{:S(2)}) async-start(), calls=%async_computation.7 | async-start | bytes 9437184 | tf_op jit(solution)/shard_map/all_gather | solution.py:98
  60.7 175.4 %all-gather.9.cloned.1.call-start = ((), (), s32[]{:S(2)}) async-start(), calls=%async_computation.8 | async-start | bytes 9437184 | tf_op jit(solution)/shard_map/all_gather | solution.py:99
  61.4 15.2 %collective-permute-start = (bf16[256,2048]{1,0:T(8,128)(2,1)S(1)}, bf16[256,2048]{1,0:T(8,128)(2,1)S(1)}, u32[]{:S(2)}, u32[]{:S(2)}) collective-permute-start(bf16[256,2048]{1,0:T(8,128)(2,1)S(1)} %copy-done.2), channel_id=1, source_target_pairs={{0,4},{4,8},{8,12},{12,16},{16,20},{20,24},{24,28},{28,0},{1,5},{5... | collective-permute-start | bytes 3145736 | tf_op jit(solution)/shard_map/ppermute | solution.py:109
  76.6 15.1 %collective-permute-start.1 = (bf16[256,2048]{1,0:T(8,128)(2,1)S(1)}, bf16[256,2048]{1,0:T(8,128)(2,1)S(1)}, u32[]{:S(2)}, u32[]{:S(2)}) collective-permute-start(bf16[256,2048]{1,0:T(8,128)(2,1)S(1)} %collective-permute-done), channel_id=1, source_target_pairs={{0,4},{4,8},{8,12},{12,16},{16,20},{20,24},{24,28},{28,0},{1,5},{5... | collective-permute-start | bytes 3145736 | tf_op jit(solution)/shard_map/ppermute | solution.py:109
  91.7 1.0 copy-start.3
  92.7 15.1 %collective-permute-start.2 = (bf16[256,2048]{1,0:T(8,128)(2,1)S(1)}, bf16[256,2048]{1,0:T(8,128)(2,1)S(1)}, u32[]{:S(2)}, u32[]{:S(2)}) collective-permute-start(bf16[256,2048]{1,0:T(8,128)(2,1)S(1)} %collective-permute-done.1), channel_id=1, source_target_pairs={{0,4},{4,8},{8,12},{12,16},{16,20},{20,24},{24,28},{28,0},{1,5},{5... | collective-permute-start | bytes 3145736 | tf_op jit(solution)/shard_map/ppermute | solution.py:109
  107.8 1.0 copy-start.5
  108.8 26.5 %collective-permute-start.3 = (bf16[256,2048]{1,0:T(8,128)(2,1)S(1)}, bf16[256,2048]{1,0:T(8,128)(2,1)}, u32[]{:S(2)}, u32[]{:S(2)}) collective-permute-start(bf16[256,2048]{1,0:T(8,128)(2,1)S(1)} %collective-permute-done.2), channel_id=1, source_target_pairs={{0,4},{4,8},{8,12},{12,16},{16,20},{20,24},{24,28},{28,0},{1,5},{5... | collective-permute-start | bytes 3145736 | tf_op jit(solution)/shard_map/ppermute | solution.py:109
  135.2 32.9 %collective-permute-start.4 = (bf16[256,2048]{1,0:T(8,128)(2,1)}, bf16[256,2048]{1,0:T(8,128)(2,1)}, u32[]{:S(2)}, u32[]{:S(2)}) collective-permute-start(bf16[256,2048]{1,0:T(8,128)(2,1)} %collective-permute-done.3), channel_id=1, source_target_pairs={{0,4},{4,8},{8,12},{12,16},{16,20},{20,24},{24,28},{28,0},{1,5},{5... | collective-permute-start | bytes 3145736 | tf_op jit(solution)/shard_map/ppermute | solution.py:109
  138.5 30.8 %all-to-all-start.3 = ((bf16[8,1,2]{2,1,0:T(2,128)(2,1)}), bf16[8,1,2]{2,1,0:T(2,128)(2,1)S(1)}, u32[]{:S(2)}, u32[]{:S(2)}) async-start(bf16[8,1,2]{2,1,0:T(2,128)(2,1)} %broadcast_in_dim.133), calls=%async_computation.3 | async-start | bytes 8192 | tf_op jit(solution)/shard_map/all_to_all | solution.py:77
  168.1 17.1 %collective-permute-start.5 = (bf16[256,2048]{1,0:T(8,128)(2,1)}, bf16[256,2048]{1,0:T(8,128)(2,1)}, u32[]{:S(2)}, u32[]{:S(2)}) collective-permute-start(bf16[256,2048]{1,0:T(8,128)(2,1)} %collective-permute-done.4), channel_id=1, source_target_pairs={{0,4},{4,8},{8,12},{12,16},{16,20},{20,24},{24,28},{28,0},{1,5},{5... | collective-permute-start | bytes 3145736 | tf_op jit(solution)/shard_map/ppermute | solution.py:109
  169.3 15.1 %all-to-all-start.2 = ((bf16[8,1,128]{2,1,0:T(2,128)(2,1)}), bf16[8,1,128]{2,1,0:T(2,128)(2,1)S(1)}, u32[]{:S(2)}, u32[]{:S(2)}) async-start(bf16[8,1,128]{2,1,0:T(2,128)(2,1)} %copy.44), calls=%async_computation.2 | async-start | bytes 8192 | tf_op jit(solution)/shard_map/all_to_all | solution.py:76
  173.3 110.5 %all-gather.11.cloned.1.call-start = ((), (), s32[]{:S(2)}) async-start(), calls=%async_computation.9 | async-start | bytes 2621440 | tf_op jit(solution)/shard_map/all_gather | solution.py:95
  185.1 179.1 %reduce-scatter.5.cloned.1.call-start = ((), (), s32[]{:S(2)}) async-start(), calls=%async_computation.11 | async-start | bytes 9437184 | tf_op jit(solution)/shard_map/reduce_scatter | solution.py:126
  185.2 109.0 %collective-permute-start.6 = (bf16[256,2048]{1,0:T(8,128)(2,1)}, bf16[256,2048]{1,0:T(8,128)(2,1)}, u32[]{:S(2)}, u32[]{:S(2)}) collective-permute-start(bf16[256,2048]{1,0:T(8,128)(2,1)} %collective-permute-done.5), channel_id=1, source_target_pairs={{0,4},{4,8},{8,12},{12,16},{16,20},{20,24},{24,28},{28,0},{1,5},{5... | collective-permute-start | bytes 3145736 | tf_op jit(solution)/shard_map/ppermute | solution.py:109
  293.9 189.7 %reduce-scatter.3.cloned.1.call-start = ((), (), s32[]{:S(2)}) async-start(), calls=%async_computation.10 | async-start | bytes 18874368 | tf_op jit(solution)/shard_map/reduce_scatter | solution.py:129
  294.2 5.5 %copy-start.6 = (bf16[256,2048]{1,0:T(8,128)(2,1)S(1)}, bf16[256,2048]{1,0:T(8,128)(2,1)}, u32[]{:S(2)}) copy-start(bf16[256,2048]{1,0:T(8,128)(2,1)} %copy-done.5) | copy-start | bytes 3145732
  295.6 4.2 copy-start.4
  305.9 1.9 copy-start.9
  307.8 6.1 %copy-start.8 = (bf16[512,2048]{1,0:T(8,128)(2,1)S(1)}, bf16[512,2048]{1,0:T(8,128)(2,1)}, u32[]{:S(2)}) copy-start(bf16[512,2048]{1,0:T(8,128)(2,1)} %all-gather.5.cloned.1.call-done) | copy-start | bytes 6291460
Sparse Core Ops, SparseCore 0:
  60.0 45.0 all-gather.4
  107.0 68.4 all-gather.6
  177.4 58.6 all-gather.8
  238.1 45.6 all-gather.10
  294.0 70.0 reduce-scatter.4
  367.6 116.0 reduce-scatter.2
